TPU v7x, 32 devices: a whole 2x2x4 slice. The times are simulated.
32 devices in a mesh: groups: 2 (over y), section: 4 (over z), seq: 4 (over x, core).
Axes of the slice: x: 2, y: 2, z: 4, core: 2. Of those that a mesh axis runs over, the one named last changes fastest.
Arguments:
- tokens: bfloat16 [8, 256, 1440], P('groups', 'seq'), parts along dimension 0, may hold values from -6 to 6
- block_order: int32 [8], P('groups'), parts along dimension 0, may hold values from 0 to 3, each once
- prompt_lengths: int32 [8], P('groups'), parts along dimension 0, may hold values from 1 to 256, 576 in all
- norm_gain: float32 [4, 1440], P('section'), may hold values from 0.1 to 1.9
- w_query: bfloat16 [4, 1440, 2048], P('section', None, 'seq'), may hold values from -4 to 4
- w_key_value: bfloat16 [4, 1440, 512], P('section'), may hold values from -4 to 4
- w_out: bfloat16 [4, 2048, 1440], P('section', 'seq'), may hold values from -0.125 to 0.125
- sink_logits: float32 [4, 32], P('section'), may hold values from 0 to 4
Outputs:
- hidden_states: bfloat16 [4, 8, 256, 1440], P('section', 'groups', 'seq'), parts along dimension 1
- layer_cache: bfloat16 [4, 8, 256, 512], P('section', 'groups', 'seq'), parts along dimension 1
There are 2 independent parts, one for each index of `groups`. A program takes and returns all parts, laid end to end along the dimension named above; an argument that names none is the same for every part. Nothing has to cross between parts.
Inputs may be any that keep to these rules, and one draw needn't show every extreme that they name: `block_order`: each of 0 to 3 exactly once. `prompt_lengths`: the longest prompt is full.
All inputs are finite; a program needn't handle non-finite values.
Results may differ from a plain program's by a relative error of at most 0.024.
Values may be sent and summed in bfloat16 or wider, within the bound.
No kernel may reach another device: no remote copies, remote signals or barrier semaphores. Data moves between devices by JAX's collectives and lax.ppermute only.
A program may use at most 128 MiB of HBM per device.

v0:
```python
import math
import jax
import jax.numpy as jnp
from jax import lax
from jax.sharding import PartitionSpec as P

HEAD_DIM = 64
WIN = 128
THETA = 150000.0
EPSILON = 1e-05


def from_behind(block, axis, distance):
    devices = range(lax.axis_size(axis))
    route = [(i - distance, i) for i in devices if i - distance in devices]
    return lax.ppermute(block, axis, route)


def rotary(positions, head_size):
    half = head_size // 2
    freq = jnp.exp(jnp.arange(half, dtype=jnp.float32) * (-2.0 * math.log(THETA) / head_size))
    angles = positions.astype(jnp.float32)[:, None] * freq[None, :]
    return (jnp.cos(angles)[:, None, :], jnp.sin(angles)[:, None, :])


def rotate(values, cosine, sine):
    half = values.shape[-1] // 2
    first = values[..., :half]
    second = values[..., half:]
    return jnp.concatenate([first * cosine - second * sine, second * cosine + first * sine], -1)


def per_device(
    tokens, block_order, prompt_lengths, norm_gain, w_query, w_key_value, w_out, sink_logits
):
    section_index = lax.axis_index("section")
    sections = lax.axis_size("section")
    seq_index = lax.axis_index("seq")
    micro, rows, width = tokens.shape
    full_query, full_out = (
        lax.all_gather(w_query, "seq", axis=2, tiled=True),
        lax.all_gather(w_out, "seq", axis=1, tiled=True),
    )
    query_weight = full_query[0]
    out_weight = full_out[0]
    pair_weight = w_key_value[0]
    gain = norm_gain[0]
    heads_width = query_weight.shape[1]
    head_count = heads_width // HEAD_DIM
    kv_width = pair_weight.shape[1] // 2
    kv_heads = kv_width // HEAD_DIM
    group = head_count // kv_heads
    sink = sink_logits[0].reshape(kv_heads, group)[:, :, None]
    keep = min(WIN, rows)
    depth = WIN // keep
    start = seq_index * rows
    positions = start + jnp.arange(rows, dtype=jnp.int32)
    cosine, sine = rotary(positions, HEAD_DIM)
    key_positions = start - WIN + jnp.arange(WIN + rows, dtype=jnp.int32)

    def project(hidden):
        widened = hidden.astype(jnp.float32)
        scale = lax.rsqrt(jnp.mean(widened * widened, -1, keepdims=True) + EPSILON)
        normed = (widened * scale * gain).astype(jnp.bfloat16)
        queries = jnp.dot(normed, query_weight, preferred_element_type=jnp.float32).reshape(
            rows, head_count, HEAD_DIM
        )
        queries = rotate(queries, cosine, sine).astype(jnp.bfloat16).reshape(rows, heads_width)
        projected = jnp.dot(normed, pair_weight, preferred_element_type=jnp.float32)
        rotated = rotate(
            projected[:, :kv_width].reshape(rows, kv_heads, HEAD_DIM), cosine, sine
        ).reshape(rows, kv_width)
        cache = jnp.concatenate([rotated, projected[:, kv_width:]], 1).astype(jnp.bfloat16)
        return (queries, cache)

    def project_spare(hidden):
        return (
            jnp.zeros((rows, heads_width), jnp.bfloat16),
            jnp.zeros((rows, 2 * kv_width), jnp.bfloat16),
        )

    def window_of(cache):
        pieces = [from_behind(cache, "seq", offset) for offset in range(depth, 0, -1)]
        return jnp.concatenate(pieces, 0)

    def attend(operands):
        hidden, queries, cache, window, length = operands
        joined = jnp.concatenate([window, cache], 0)
        key_heads = joined[:, :kv_width].reshape(WIN + rows, kv_heads, HEAD_DIM)
        value_heads = joined[:, kv_width:].reshape(WIN + rows, kv_heads, HEAD_DIM)
        grouped = queries.reshape(rows, kv_heads, group, HEAD_DIM)
        scores = (
            jnp.einsum("qkgd,skd->kgqs", grouped, key_heads, preferred_element_type=jnp.float32)
            * 0.125
        )
        query_col = positions[:, None]
        key_row = key_positions[None, :]
        allowed = (key_row <= query_col) & (query_col - key_row < WIN) & (key_row >= 0)
        allowed = allowed & ((key_row < length) | (key_row == query_col))
        masked = jnp.where(allowed, scores, jnp.float32(-1e30))
        top = jnp.maximum(jnp.max(masked, -1), sink)
        expo = jnp.where(allowed, jnp.exp(scores - top[..., None]), jnp.float32(0.0))
        total = jnp.sum(expo, -1) + jnp.exp(sink - top)
        weights = (expo / total[..., None]).astype(jnp.bfloat16)
        context = jnp.einsum(
            "kgqs,skd->qkgd", weights, value_heads, preferred_element_type=jnp.float32
        )
        context = context.reshape(rows, heads_width).astype(jnp.bfloat16)
        output = jnp.dot(context, out_weight, preferred_element_type=jnp.float32)
        return (hidden.astype(jnp.float32) + output).astype(jnp.bfloat16)

    def pass_through(operands):
        return operands[0]

    def turn(counter, carry):
        arriving, hidden_buffer, cache_buffer = carry
        slot = counter - section_index
        active = (slot >= 0) & (slot < micro)
        slot_safe = jnp.clip(slot, 0, micro - 1)
        block = block_order[slot_safe]
        length = prompt_lengths[block]
        entering = lax.dynamic_index_in_dim(tokens, block, 0, keepdims=False)
        hidden = jnp.where(section_index == 0, entering, arriving)
        queries, cache = lax.cond(active, project, project_spare, hidden)
        window = window_of(cache)
        updated = lax.cond(active, attend, pass_through, (hidden, queries, cache, window, length))
        previous_hidden = lax.dynamic_index_in_dim(hidden_buffer, slot_safe, 0, keepdims=False)
        previous_cache = lax.dynamic_index_in_dim(cache_buffer, slot_safe, 0, keepdims=False)
        hidden_buffer = lax.dynamic_update_index_in_dim(
            hidden_buffer, jnp.where(active, updated, previous_hidden), slot_safe, 0
        )
        cache_buffer = lax.dynamic_update_index_in_dim(
            cache_buffer, jnp.where(active, cache, previous_cache), slot_safe, 0
        )
        passed = from_behind(updated, "section", 1)
        return (passed, hidden_buffer, cache_buffer)

    initial = (
        jnp.zeros((rows, width), jnp.bfloat16),
        jnp.zeros((micro, rows, width), jnp.bfloat16),
        jnp.zeros((micro, rows, 2 * kv_width), jnp.bfloat16),
    )
    final = lax.fori_loop(0, micro + sections - 1, turn, initial)
    return (final[1][None], final[2][None])


def solution(mesh):
    in_specs = (
        P("groups", "seq", None),
        P("groups"),
        P("groups"),
        P("section", None),
        P("section", None, "seq"),
        P("section", None, None),
        P("section", "seq", None),
        P("section", None),
    )
    out_specs = (P("section", "groups", "seq", None), P("section", "groups", "seq", None))
    return jax.shard_map(
        per_device, mesh=mesh, in_specs=in_specs, out_specs=out_specs, check_vma=False
    )
```

profile of v0, /device:TPU:28, one launch (start us, length us, event | category | flops | bytes accessed | tf_op | source)
XLA Modules:
  0.0 363.9 jit_solution(2830805438816558788)
XLA Ops:
  11.5 43.2 %all-gather.3.cloned.1.call-done = bf16[1,1440,2048]{2,1,0:T(8,128)(2,1)} async-done(((bf16[1,1440,512]{2,1,0:T(8,128)(2,1)}), bf16[1,1440,2048]{2,1,0:T(8,128)(2,1)}) %all-gather.3.cloned.1.call-update) | async-done | bytes 5898256 | tf_op jit(solution)/shard_map/all_gather | solution.py:41
  54.6 47.9 %all-gather.5.cloned.1.call-done = bf16[1,2048,1440]{2,1,0:T(8,128)(2,1)} async-done(((bf16[1,512,1440]{2,1,0:T(8,128)(2,1)}), bf16[1,2048,1440]{2,1,0:T(8,128)(2,1)}) %all-gather.5.cloned.1.call-update) | async-done | bytes 5898256 | tf_op jit(solution)/shard_map/all_gather | solution.py:42
  104.3 252.8 %while.20 = (s32[]{:T(128)}, bf16[64,1440]{1,0:T(8,128)(2,1)S(1)}, bf16[4,64,1440]{2,1,0:T(8,128)(2,1)}, bf16[4,64,512]{2,1,0:T(8,128)(2,1)}, s32[]{:T(128)}, /*...) while((s32[]{:T(128)}, bf16[64,1440]{1,0:T(8,128)(2,1)S(1)}, ...), condition=%wide.region_8.9_spmd.clone.clone, body=%wide.region_0.8_spmd.clone.clone.sunk | while | flops 958372544 | bytes 47880768 | solution.py:143
  118.0 7.3 %collective-permute-done.2 = bf16[64,1440]{1,0:T(8,128)(2,1)S(1)} collective-permute-done((bf16[64,1440]{1,0:T(8,128)(2,1)S(1)}, bf16[64,1440]{1,0:T(8,128)(2,1)S(1)}, u32[]{:S(2)}, u32[]{:S(2)}) %collective-permute-start.2) | collective-permute-done | bytes 184352 | tf_op jit(solution)/shard_map/while/body/eval_jaxpr/ppermute | solution.py:16
  130.1 3.0 collective-permute-start
  139.0 7.2 %collective-permute-done.2 = bf16[64,1440]{1,0:T(8,128)(2,1)S(1)} collective-permute-done((bf16[64,1440]{1,0:T(8,128)(2,1)S(1)}, bf16[64,1440]{1,0:T(8,128)(2,1)S(1)}, u32[]{:S(2)}, u32[]{:S(2)}) %collective-permute-start.2) | collective-permute-done | bytes 184352 | tf_op jit(solution)/shard_map/while/body/eval_jaxpr/ppermute | solution.py:16
  151.0 3.0 collective-permute-start
  159.8 50.5 %collective-permute-done.2 = bf16[64,1440]{1,0:T(8,128)(2,1)S(1)} collective-permute-done((bf16[64,1440]{1,0:T(8,128)(2,1)S(1)}, bf16[64,1440]{1,0:T(8,128)(2,1)S(1)}, u32[]{:S(2)}, u32[]{:S(2)}) %collective-permute-start.2) | collective-permute-done | bytes 184352 | tf_op jit(solution)/shard_map/while/body/eval_jaxpr/ppermute | solution.py:16
  213.8 9.2 %conditional.8 = (bf16[64,2048]{1,0:T(8,128)(2,1)S(1)}, bf16[64,512]{1,0:T(8,128)(2,1)}, bf16[64,512]{0,1:T(8,128)(2,1)}) conditional(s32[]{:T(128)} %convert_element_type.69, () %tuple.79, (bf16[64,1440]{1,0:T(8,128)(2,1)S(1)}, f32[1,1440]{1,0:T(1,128)S(1)}, bf16[1440,2048]{1,0:T(8,128)(2,1)}, f32[64,1,32]{2,0,1:T(8,128)S(1)}, ...), branch_computations={%region_1.1_spmd, %region_2.3_spmd} | conditional | flops 474183744 | bytes 12373788 | solution.py:124
  214.0 3.9 %fusion.26 = f32[64,2048]{1,0:T(8,128)S(1)} fusion(bf16[1440,2048]{1,0:T(8,128)(2,1)} %get-tuple-element.374, bf16[64,1440]{1,0:T(8,128)(2,1)S(1)} %get-tuple-element.372, f32[1440]{0:T(1024)S(1)} %reduce, f32[64]{0:T(128)S(1)} %add_rsqrt_fusion), kind=kOutput, calls=%fused_computation.44 | convolution fusion | flops 377856000 | bytes 6612864 | tf_op jit(solution)/shard_map/while/body/eval_jaxpr/cond/branch_1_fun/dot_general | solution.py:65
  230.0 8.0 %conditional.9 = (bf16[64,1440]{1,0:T(8,128)(2,1)S(1)}) conditional(s32[]{:T(128)} %convert_element_type.69, bf16[64,1440]{1,0:T(8,128)(2,1)S(1)} %bitcast_select_fusion.5, (bf16[64,1440]{1,0:T(8,128)(2,1)S(1)}, bf16[64,512]{0,1:T(8,128)(2,1)S(1)}, bf16[64,512]{0,1:T(8,128)(2,1)S(1)}, bf16[64,512]{1,0:T(8,128)(2,1)}, s32[]{:T(128)}, ...), branch_computations={%region_4.4_spmd, %region_5.7_spmd} | conditional | flops 483969664 | bytes 32420688 | solution.py:126
  240.0 7.1 %collective-permute-done.2 = bf16[64,1440]{1,0:T(8,128)(2,1)S(1)} collective-permute-done((bf16[64,1440]{1,0:T(8,128)(2,1)S(1)}, bf16[64,1440]{1,0:T(8,128)(2,1)S(1)}, u32[]{:S(2)}, u32[]{:S(2)}) %collective-permute-start.2) | collective-permute-done | bytes 184352 | tf_op jit(solution)/shard_map/while/body/eval_jaxpr/ppermute | solution.py:16
  250.6 9.2 %conditional.8 = (bf16[64,2048]{1,0:T(8,128)(2,1)S(1)}, bf16[64,512]{1,0:T(8,128)(2,1)}, bf16[64,512]{0,1:T(8,128)(2,1)}) conditional(s32[]{:T(128)} %convert_element_type.69, () %tuple.79, (bf16[64,1440]{1,0:T(8,128)(2,1)S(1)}, f32[1,1440]{1,0:T(1,128)S(1)}, bf16[1440,2048]{1,0:T(8,128)(2,1)}, f32[64,1,32]{2,0,1:T(8,128)S(1)}, ...), branch_computations={%region_1.1_spmd, %region_2.3_spmd} | conditional | flops 474183744 | bytes 12373788 | solution.py:124
  250.8 3.9 %fusion.26 = f32[64,2048]{1,0:T(8,128)S(1)} fusion(bf16[1440,2048]{1,0:T(8,128)(2,1)} %get-tuple-element.374, bf16[64,1440]{1,0:T(8,128)(2,1)S(1)} %get-tuple-element.372, f32[1440]{0:T(1024)S(1)} %reduce, f32[64]{0:T(128)S(1)} %add_rsqrt_fusion), kind=kOutput, calls=%fused_computation.44 | convolution fusion | flops 377856000 | bytes 6612864 | tf_op jit(solution)/shard_map/while/body/eval_jaxpr/cond/branch_1_fun/dot_general | solution.py:65
  266.7 8.0 %conditional.9 = (bf16[64,1440]{1,0:T(8,128)(2,1)S(1)}) conditional(s32[]{:T(128)} %convert_element_type.69, bf16[64,1440]{1,0:T(8,128)(2,1)S(1)} %bitcast_select_fusion.5, (bf16[64,1440]{1,0:T(8,128)(2,1)S(1)}, bf16[64,512]{0,1:T(8,128)(2,1)S(1)}, bf16[64,512]{0,1:T(8,128)(2,1)S(1)}, bf16[64,512]{1,0:T(8,128)(2,1)}, s32[]{:T(128)}, ...), branch_computations={%region_4.4_spmd, %region_5.7_spmd} | conditional | flops 483969664 | bytes 32420688 | solution.py:126
  276.8 7.1 %collective-permute-done.2 = bf16[64,1440]{1,0:T(8,128)(2,1)S(1)} collective-permute-done((bf16[64,1440]{1,0:T(8,128)(2,1)S(1)}, bf16[64,1440]{1,0:T(8,128)(2,1)S(1)}, u32[]{:S(2)}, u32[]{:S(2)}) %collective-permute-start.2) | collective-permute-done | bytes 184352 | tf_op jit(solution)/shard_map/while/body/eval_jaxpr/ppermute | solution.py:16
  287.3 9.2 %conditional.8 = (bf16[64,2048]{1,0:T(8,128)(2,1)S(1)}, bf16[64,512]{1,0:T(8,128)(2,1)}, bf16[64,512]{0,1:T(8,128)(2,1)}) conditional(s32[]{:T(128)} %convert_element_type.69, () %tuple.79, (bf16[64,1440]{1,0:T(8,128)(2,1)S(1)}, f32[1,1440]{1,0:T(1,128)S(1)}, bf16[1440,2048]{1,0:T(8,128)(2,1)}, f32[64,1,32]{2,0,1:T(8,128)S(1)}, ...), branch_computations={%region_1.1_spmd, %region_2.3_spmd} | conditional | flops 474183744 | bytes 12373788 | solution.py:124
  287.5 3.9 %fusion.26 = f32[64,2048]{1,0:T(8,128)S(1)} fusion(bf16[1440,2048]{1,0:T(8,128)(2,1)} %get-tuple-element.374, bf16[64,1440]{1,0:T(8,128)(2,1)S(1)} %get-tuple-element.372, f32[1440]{0:T(1024)S(1)} %reduce, f32[64]{0:T(128)S(1)} %add_rsqrt_fusion), kind=kOutput, calls=%fused_computation.44 | convolution fusion | flops 377856000 | bytes 6612864 | tf_op jit(solution)/shard_map/while/body/eval_jaxpr/cond/branch_1_fun/dot_general | solution.py:65
  303.5 8.0 %conditional.9 = (bf16[64,1440]{1,0:T(8,128)(2,1)S(1)}) conditional(s32[]{:T(128)} %convert_element_type.69, bf16[64,1440]{1,0:T(8,128)(2,1)S(1)} %bitcast_select_fusion.5, (bf16[64,1440]{1,0:T(8,128)(2,1)S(1)}, bf16[64,512]{0,1:T(8,128)(2,1)S(1)}, bf16[64,512]{0,1:T(8,128)(2,1)S(1)}, bf16[64,512]{1,0:T(8,128)(2,1)}, s32[]{:T(128)}, ...), branch_computations={%region_4.4_spmd, %region_5.7_spmd} | conditional | flops 483969664 | bytes 32420688 | solution.py:126
  313.5 7.1 %collective-permute-done.2 = bf16[64,1440]{1,0:T(8,128)(2,1)S(1)} collective-permute-done((bf16[64,1440]{1,0:T(8,128)(2,1)S(1)}, bf16[64,1440]{1,0:T(8,128)(2,1)S(1)}, u32[]{:S(2)}, u32[]{:S(2)}) %collective-permute-start.2) | collective-permute-done | bytes 184352 | tf_op jit(solution)/shard_map/while/body/eval_jaxpr/ppermute | solution.py:16
  324.1 9.2 %conditional.8 = (bf16[64,2048]{1,0:T(8,128)(2,1)S(1)}, bf16[64,512]{1,0:T(8,128)(2,1)}, bf16[64,512]{0,1:T(8,128)(2,1)}) conditional(s32[]{:T(128)} %convert_element_type.69, () %tuple.79, (bf16[64,1440]{1,0:T(8,128)(2,1)S(1)}, f32[1,1440]{1,0:T(1,128)S(1)}, bf16[1440,2048]{1,0:T(8,128)(2,1)}, f32[64,1,32]{2,0,1:T(8,128)S(1)}, ...), branch_computations={%region_1.1_spmd, %region_2.3_spmd} | conditional | flops 474183744 | bytes 12373788 | solution.py:124
  324.3 3.9 %fusion.26 = f32[64,2048]{1,0:T(8,128)S(1)} fusion(bf16[1440,2048]{1,0:T(8,128)(2,1)} %get-tuple-element.374, bf16[64,1440]{1,0:T(8,128)(2,1)S(1)} %get-tuple-element.372, f32[1440]{0:T(1024)S(1)} %reduce, f32[64]{0:T(128)S(1)} %add_rsqrt_fusion), kind=kOutput, calls=%fused_computation.44 | convolution fusion | flops 377856000 | bytes 6612864 | tf_op jit(solution)/shard_map/while/body/eval_jaxpr/cond/branch_1_fun/dot_general | solution.py:65
  340.2 8.0 %conditional.9 = (bf16[64,1440]{1,0:T(8,128)(2,1)S(1)}) conditional(s32[]{:T(128)} %convert_element_type.69, bf16[64,1440]{1,0:T(8,128)(2,1)S(1)} %bitcast_select_fusion.5, (bf16[64,1440]{1,0:T(8,128)(2,1)S(1)}, bf16[64,512]{0,1:T(8,128)(2,1)S(1)}, bf16[64,512]{0,1:T(8,128)(2,1)S(1)}, bf16[64,512]{1,0:T(8,128)(2,1)}, s32[]{:T(128)}, ...), branch_computations={%region_4.4_spmd, %region_5.7_spmd} | conditional | flops 483969664 | bytes 32420688 | solution.py:126
  350.3 6.8 %collective-permute-done.2 = bf16[64,1440]{1,0:T(8,128)(2,1)S(1)} collective-permute-done((bf16[64,1440]{1,0:T(8,128)(2,1)S(1)}, bf16[64,1440]{1,0:T(8,128)(2,1)S(1)}, u32[]{:S(2)}, u32[]{:S(2)}) %collective-permute-start.2) | collective-permute-done | bytes 184352 | tf_op jit(solution)/shard_map/while/body/eval_jaxpr/ppermute | solution.py:16
  (284 shorter events, 134.1 us)
Async XLA Ops:
  7.2 47.5 %all-gather.3.cloned.1.call-start = ((), (), s32[]{:S(2)}) async-start(), calls=%async_computation | async-start | bytes 7372800 | tf_op jit(solution)/shard_map/all_gather | solution.py:41
  7.9 94.7 %all-gather.5.cloned.1.call-start = ((), (), s32[]{:S(2)}) async-start(), calls=%async_computation.1 | async-start | bytes 7864320 | tf_op jit(solution)/shard_map/all_gather | solution.py:42
  10.2 94.1 %copy-start.5 = (s32[4]{0:T(128)S(1)}, s32[4]{0:T(128)}, u32[]{:S(2)}) copy-start(s32[4]{0:T(128)} %param.16) | copy-start | bytes 52
  109.1 6.8 %collective-permute-start = (bf16[64,512]{0,1:T(8,128)(2,1)}, bf16[64,512]{0,1:T(8,128)(2,1)S(1)}, u32[]{:S(2)}, u32[]{:S(2)}) collective-permute-start(bf16[64,512]{0,1:T(8,128)(2,1)} %get-tuple-element.696), channel_id=1, source_target_pairs={{0,2},{1,3},{4,6},{5,7},{8,10},{9,11},{12,14},{13,15},{16,18},{17,... | collective-permute-start | bytes 196616 | tf_op jit(solution)/shard_map/while/body/eval_jaxpr/ppermute | solution.py:16
  111.6 4.3 %collective-permute-start.1 = (bf16[64,512]{0,1:T(8,128)(2,1)}, bf16[64,512]{0,1:T(8,128)(2,1)S(1)}, u32[]{:S(2)}, u32[]{:S(2)}) collective-permute-start(bf16[64,512]{0,1:T(8,128)(2,1)} %get-tuple-element.696), channel_id=1, source_target_pairs={{0,1},{1,2},{2,3},{4,5},{5,6},{6,7},{8,9},{9,10},{10,11},{12,13},{... | collective-permute-start | bytes 196616 | tf_op jit(solution)/shard_map/while/body/eval_jaxpr/ppermute | solution.py:16
  116.0 9.3 %collective-permute-start.2 = (bf16[64,1440]{1,0:T(8,128)(2,1)S(1)}, bf16[64,1440]{1,0:T(8,128)(2,1)S(1)}, u32[]{:S(2)}, u32[]{:S(2)}) collective-permute-start(bf16[64,1440]{1,0:T(8,128)(2,1)S(1)} %get-tuple-element.771), channel_id=1, source_target_pairs={{0,4},{4,8},{8,12},{1,5},{5,9},{9,13},{2,6},{6,10},{10,14},{3,7},{... | collective-permute-start | bytes 552968 | tf_op jit(solution)/shard_map/while/body/eval_jaxpr/ppermute | solution.py:16
  130.1 6.8 %collective-permute-start = (bf16[64,512]{0,1:T(8,128)(2,1)}, bf16[64,512]{0,1:T(8,128)(2,1)S(1)}, u32[]{:S(2)}, u32[]{:S(2)}) collective-permute-start(bf16[64,512]{0,1:T(8,128)(2,1)} %get-tuple-element.696), channel_id=1, source_target_pairs={{0,2},{1,3},{4,6},{5,7},{8,10},{9,11},{12,14},{13,15},{16,18},{17,... | collective-permute-start | bytes 196616 | tf_op jit(solution)/shard_map/while/body/eval_jaxpr/ppermute | solution.py:16
  133.2 3.8 %collective-permute-start.1 = (bf16[64,512]{0,1:T(8,128)(2,1)}, bf16[64,512]{0,1:T(8,128)(2,1)S(1)}, u32[]{:S(2)}, u32[]{:S(2)}) collective-permute-start(bf16[64,512]{0,1:T(8,128)(2,1)} %get-tuple-element.696), channel_id=1, source_target_pairs={{0,1},{1,2},{2,3},{4,5},{5,6},{6,7},{8,9},{9,10},{10,11},{12,13},{... | collective-permute-start | bytes 196616 | tf_op jit(solution)/shard_map/while/body/eval_jaxpr/ppermute | solution.py:16
  137.0 9.2 %collective-permute-start.2 = (bf16[64,1440]{1,0:T(8,128)(2,1)S(1)}, bf16[64,1440]{1,0:T(8,128)(2,1)S(1)}, u32[]{:S(2)}, u32[]{:S(2)}) collective-permute-start(bf16[64,1440]{1,0:T(8,128)(2,1)S(1)} %get-tuple-element.771), channel_id=1, source_target_pairs={{0,4},{4,8},{8,12},{1,5},{5,9},{9,13},{2,6},{6,10},{10,14},{3,7},{... | collective-permute-start | bytes 552968 | tf_op jit(solution)/shard_map/while/body/eval_jaxpr/ppermute | solution.py:16
  151.0 6.8 %collective-permute-start = (bf16[64,512]{0,1:T(8,128)(2,1)}, bf16[64,512]{0,1:T(8,128)(2,1)S(1)}, u32[]{:S(2)}, u32[]{:S(2)}) collective-permute-start(bf16[64,512]{0,1:T(8,128)(2,1)} %get-tuple-element.696), channel_id=1, source_target_pairs={{0,2},{1,3},{4,6},{5,7},{8,10},{9,11},{12,14},{13,15},{16,18},{17,... | collective-permute-start | bytes 196616 | tf_op jit(solution)/shard_map/while/body/eval_jaxpr/ppermute | solution.py:16
  154.0 3.8 %collective-permute-start.1 = (bf16[64,512]{0,1:T(8,128)(2,1)}, bf16[64,512]{0,1:T(8,128)(2,1)S(1)}, u32[]{:S(2)}, u32[]{:S(2)}) collective-permute-start(bf16[64,512]{0,1:T(8,128)(2,1)} %get-tuple-element.696), channel_id=1, source_target_pairs={{0,1},{1,2},{2,3},{4,5},{5,6},{6,7},{8,9},{9,10},{10,11},{12,13},{... | collective-permute-start | bytes 196616 | tf_op jit(solution)/shard_map/while/body/eval_jaxpr/ppermute | solution.py:16
  157.8 52.5 %collective-permute-start.2 = (bf16[64,1440]{1,0:T(8,128)(2,1)S(1)}, bf16[64,1440]{1,0:T(8,128)(2,1)S(1)}, u32[]{:S(2)}, u32[]{:S(2)}) collective-permute-start(bf16[64,1440]{1,0:T(8,128)(2,1)S(1)} %get-tuple-element.771), channel_id=1, source_target_pairs={{0,4},{4,8},{8,12},{1,5},{5,9},{9,13},{2,6},{6,10},{10,14},{3,7},{... | collective-permute-start | bytes 552968 | tf_op jit(solution)/shard_map/while/body/eval_jaxpr/ppermute | solution.py:16
  223.0 6.9 %collective-permute-start = (bf16[64,512]{0,1:T(8,128)(2,1)}, bf16[64,512]{0,1:T(8,128)(2,1)S(1)}, u32[]{:S(2)}, u32[]{:S(2)}) collective-permute-start(bf16[64,512]{0,1:T(8,128)(2,1)} %get-tuple-element.696), channel_id=1, source_target_pairs={{0,2},{1,3},{4,6},{5,7},{8,10},{9,11},{12,14},{13,15},{16,18},{17,... | collective-permute-start | bytes 196616 | tf_op jit(solution)/shard_map/while/body/eval_jaxpr/ppermute | solution.py:16
  225.4 4.6 %collective-permute-start.1 = (bf16[64,512]{0,1:T(8,128)(2,1)}, bf16[64,512]{0,1:T(8,128)(2,1)S(1)}, u32[]{:S(2)}, u32[]{:S(2)}) collective-permute-start(bf16[64,512]{0,1:T(8,128)(2,1)} %get-tuple-element.696), channel_id=1, source_target_pairs={{0,1},{1,2},{2,3},{4,5},{5,6},{6,7},{8,9},{9,10},{10,11},{12,13},{... | collective-permute-start | bytes 196616 | tf_op jit(solution)/shard_map/while/body/eval_jaxpr/ppermute | solution.py:16
  238.0 9.1 %collective-permute-start.2 = (bf16[64,1440]{1,0:T(8,128)(2,1)S(1)}, bf16[64,1440]{1,0:T(8,128)(2,1)S(1)}, u32[]{:S(2)}, u32[]{:S(2)}) collective-permute-start(bf16[64,1440]{1,0:T(8,128)(2,1)S(1)} %get-tuple-element.771), channel_id=1, source_target_pairs={{0,4},{4,8},{8,12},{1,5},{5,9},{9,13},{2,6},{6,10},{10,14},{3,7},{... | collective-permute-start | bytes 552968 | tf_op jit(solution)/shard_map/while/body/eval_jaxpr/ppermute | solution.py:16
  259.8 6.9 %collective-permute-start = (bf16[64,512]{0,1:T(8,128)(2,1)}, bf16[64,512]{0,1:T(8,128)(2,1)S(1)}, u32[]{:S(2)}, u32[]{:S(2)}) collective-permute-start(bf16[64,512]{0,1:T(8,128)(2,1)} %get-tuple-element.696), channel_id=1, source_target_pairs={{0,2},{1,3},{4,6},{5,7},{8,10},{9,11},{12,14},{13,15},{16,18},{17,... | collective-permute-start | bytes 196616 | tf_op jit(solution)/shard_map/while/body/eval_jaxpr/ppermute | solution.py:16
  262.1 4.6 %collective-permute-start.1 = (bf16[64,512]{0,1:T(8,128)(2,1)}, bf16[64,512]{0,1:T(8,128)(2,1)S(1)}, u32[]{:S(2)}, u32[]{:S(2)}) collective-permute-start(bf16[64,512]{0,1:T(8,128)(2,1)} %get-tuple-element.696), channel_id=1, source_target_pairs={{0,1},{1,2},{2,3},{4,5},{5,6},{6,7},{8,9},{9,10},{10,11},{12,13},{... | collective-permute-start | bytes 196616 | tf_op jit(solution)/shard_map/while/body/eval_jaxpr/ppermute | solution.py:16
  274.7 9.1 %collective-permute-start.2 = (bf16[64,1440]{1,0:T(8,128)(2,1)S(1)}, bf16[64,1440]{1,0:T(8,128)(2,1)S(1)}, u32[]{:S(2)}, u32[]{:S(2)}) collective-permute-start(bf16[64,1440]{1,0:T(8,128)(2,1)S(1)} %get-tuple-element.771), channel_id=1, source_target_pairs={{0,4},{4,8},{8,12},{1,5},{5,9},{9,13},{2,6},{6,10},{10,14},{3,7},{... | collective-permute-start | bytes 552968 | tf_op jit(solution)/shard_map/while/body/eval_jaxpr/ppermute | solution.py:16
  296.5 6.9 %collective-permute-start = (bf16[64,512]{0,1:T(8,128)(2,1)}, bf16[64,512]{0,1:T(8,128)(2,1)S(1)}, u32[]{:S(2)}, u32[]{:S(2)}) collective-permute-start(bf16[64,512]{0,1:T(8,128)(2,1)} %get-tuple-element.696), channel_id=1, source_target_pairs={{0,2},{1,3},{4,6},{5,7},{8,10},{9,11},{12,14},{13,15},{16,18},{17,... | collective-permute-start | bytes 196616 | tf_op jit(solution)/shard_map/while/body/eval_jaxpr/ppermute | solution.py:16
  298.9 4.6 %collective-permute-start.1 = (bf16[64,512]{0,1:T(8,128)(2,1)}, bf16[64,512]{0,1:T(8,128)(2,1)S(1)}, u32[]{:S(2)}, u32[]{:S(2)}) collective-permute-start(bf16[64,512]{0,1:T(8,128)(2,1)} %get-tuple-element.696), channel_id=1, source_target_pairs={{0,1},{1,2},{2,3},{4,5},{5,6},{6,7},{8,9},{9,10},{10,11},{12,13},{... | collective-permute-start | bytes 196616 | tf_op jit(solution)/shard_map/while/body/eval_jaxpr/ppermute | solution.py:16
  311.5 9.1 %collective-permute-start.2 = (bf16[64,1440]{1,0:T(8,128)(2,1)S(1)}, bf16[64,1440]{1,0:T(8,128)(2,1)S(1)}, u32[]{:S(2)}, u32[]{:S(2)}) collective-permute-start(bf16[64,1440]{1,0:T(8,128)(2,1)S(1)} %get-tuple-element.771), channel_id=1, source_target_pairs={{0,4},{4,8},{8,12},{1,5},{5,9},{9,13},{2,6},{6,10},{10,14},{3,7},{... | collective-permute-start | bytes 552968 | tf_op jit(solution)/shard_map/while/body/eval_jaxpr/ppermute | solution.py:16
  333.3 6.9 %collective-permute-start = (bf16[64,512]{0,1:T(8,128)(2,1)}, bf16[64,512]{0,1:T(8,128)(2,1)S(1)}, u32[]{:S(2)}, u32[]{:S(2)}) collective-permute-start(bf16[64,512]{0,1:T(8,128)(2,1)} %get-tuple-element.696), channel_id=1, source_target_pairs={{0,2},{1,3},{4,6},{5,7},{8,10},{9,11},{12,14},{13,15},{16,18},{17,... | collective-permute-start | bytes 196616 | tf_op jit(solution)/shard_map/while/body/eval_jaxpr/ppermute | solution.py:16
  335.6 4.6 %collective-permute-start.1 = (bf16[64,512]{0,1:T(8,128)(2,1)}, bf16[64,512]{0,1:T(8,128)(2,1)S(1)}, u32[]{:S(2)}, u32[]{:S(2)}) collective-permute-start(bf16[64,512]{0,1:T(8,128)(2,1)} %get-tuple-element.696), channel_id=1, source_target_pairs={{0,1},{1,2},{2,3},{4,5},{5,6},{6,7},{8,9},{9,10},{10,11},{12,13},{... | collective-permute-start | bytes 196616 | tf_op jit(solution)/shard_map/while/body/eval_jaxpr/ppermute | solution.py:16
  348.2 8.8 %collective-permute-start.2 = (bf16[64,1440]{1,0:T(8,128)(2,1)S(1)}, bf16[64,1440]{1,0:T(8,128)(2,1)S(1)}, u32[]{:S(2)}, u32[]{:S(2)}) collective-permute-start(bf16[64,1440]{1,0:T(8,128)(2,1)S(1)} %get-tuple-element.771), channel_id=1, source_target_pairs={{0,4},{4,8},{8,12},{1,5},{5,9},{9,13},{2,6},{6,10},{10,14},{3,7},{... | collective-permute-start | bytes 552968 | tf_op jit(solution)/shard_map/while/body/eval_jaxpr/ppermute | solution.py:16
  (13 other events, 304.1 us)
Sparse Core Ops, SparseCore 0:
  9.5 45.0 all-gather.2
  56.2 46.3 all-gather.4
where the time goes:
time: 366 us; the launch traced here: 364 us
  waiting for transfers between devices  185 us (51%)
  local copies, waits for them, and re-layouts  49.8 us (14%)
  starting transfers between devices  36.5 us (10%)
  other arithmetic  35.7 us (10%)
  matrix products  28.7 us (8%)
  loops' own time  14.3 us (4%)
  between operations  14.1 us (4%)
    ppermute x21, waiting for transfers between devices, from_behind(): return lax.ppermute(block, axis, route)  92.9 us
    all_gather x1, waiting for transfers between devices, per_device(): lax.all_gather(w_out, 'seq', axis=1, tiled=True)  47.9 us
    all_gather x1, waiting for transfers between devices, per_device(): lax.all_gather(w_query, 'seq', axis=2, tiled=True)  43.2 us
    ppermute x21, starting transfers between devices, from_behind(): return lax.ppermute(block, axis, route)  36.5 us
    dot_general x4, matrix products, project(): jnp.dot(normed, query_weight, preferred_element_type=jnp.float32)  15.5 us
    another operation x1, loops' own time, per_device(): final = lax.fori_loop(0, micro + sections - 1, turn, initial)  13.4 us
    dynamic_update_slice x7, other arithmetic, turn(): lax.dynamic_update_index_in_dim(cache_buffer, jnp.where(active, cache, pr...  7.9 us
    another operation x13, local copies, waits for them, and re-layouts  7.83 us
  transfers between devices with their start and end apart: 23, of which 9 were waited for; matrix products, arithmetic and copies ran while one was open for 8% of the time, Pallas kernels for 0%

commit v1 on v0

--- a/solution.py
+++ b/solution.py
@@ -39,7 +39,9 @@
     micro, rows, width = tokens.shape
     full_query, full_out = (
         lax.all_gather(w_query, "seq", axis=2, tiled=True),
-        lax.all_gather(w_out, "seq", axis=1, tiled=True),
+        jnp.concatenate(
+            lax.all_to_all(jnp.stack([w_out] * lax.axis_size("seq")), "seq", 0, 0), axis=1
+        ),
     )
     query_weight = full_query[0]
     out_weight = full_out[0]

time: 366 us -> 378 us (1.033)
  local copies, waits for them, and re-layouts: 49.8 us -> 59.4 us
  starting transfers between devices: 36.5 us -> 43.1 us
  other arithmetic: 35.7 us -> 29.4 us
  waiting for transfers between devices: 185 us -> 189 us
    all_to_all x0 -> x1, waiting for transfers between devices: none -> 96.7 us  [per_device(): lax.all_to_all(jnp.stack([w_out] * lax.axis_size('seq')), 'seq', 0, 0)]
    all_gather x1 -> x0, waiting for transfers between devices: 47.9 us -> none  [per_device(): lax.all_gather(w_out, 'seq', axis=1, tiled=True)]
    all_gather x1, waiting for transfers between devices: 43.2 us -> 0.01 us  [per_device(): lax.all_gather(w_query, 'seq', axis=2, tiled=True)]
    unnamed x14, local copies, waits for them, and re-layouts: 2.72 us -> 9.61 us
    all_to_all x0 -> x1, starting transfers between devices: none -> 5.38 us  [per_device(): lax.all_to_all(jnp.stack([w_out] * lax.axis_size('seq')), 'seq', 0, 0)]
    reshape x4, local copies, waits for them, and re-layouts: 2.05 us -> 5.87 us  [attend(): grouped = queries.reshape(rows, kv_heads, group, HEAD_DIM)]
    another operation x13 -> x14, local copies, waits for them, and re-layouts: 7.83 us -> 7.66 us
  transfers between devices with their start and end apart: 23 -> 23, of which waited for: 9 -> 8; matrix products, arithmetic and copies ran while one was open for 8% -> 9% of each run, Pallas kernels for 0% -> 0%
where the time goes in v1:
time: 378 us; the launch traced here: 376 us
  waiting for transfers between devices  189 us (50%)
  local copies, waits for them, and re-layouts  59.4 us (16%)
  starting transfers between devices  43.1 us (11%)
  other arithmetic  29.4 us (8%)
  matrix products  28.7 us (8%)
  between operations  14.1 us (4%)
  loops' own time  13 us (3%)
    all_to_all x1, waiting for transfers between devices, per_device(): lax.all_to_all(jnp.stack([w_out] * lax.axis_size('seq')), 'seq', 0, 0)  96.7 us
    ppermute x21, waiting for transfers between devices, from_behind(): return lax.ppermute(block, axis, route)  91.2 us
    ppermute x21, starting transfers between devices, from_behind(): return lax.ppermute(block, axis, route)  37.7 us
    dot_general x4, matrix products, project(): jnp.dot(normed, query_weight, preferred_element_type=jnp.float32)  15.5 us
    another operation x1, loops' own time, per_device(): final = lax.fori_loop(0, micro + sections - 1, turn, initial)  12 us
    unnamed x14, local copies, waits for them, and re-layouts  9.61 us
  transfers between devices with their start and end apart: 23, of which 8 were waited for; matrix products, arithmetic and copies ran while one was open for 9% of the time, Pallas kernels for 0%

profile of v1, /device:TPU:28, one launch (start us, length us, event | category | flops | bytes accessed | tf_op | source)
XLA Modules:
  0.0 376.3 jit_solution(10556941721461217246)
XLA Ops:
  11.5 5.4 %all-to-all-start = ((bf16[4,1,512,1440]{2,3,1,0:T(8,128)(2,1)}), bf16[4,1,512,1440]{2,3,1,0:T(8,128)(2,1)}, u32[]{:S(2)}, u32[]{:S(2)}) async-start(bf16[4,1,512,1440]{2,3,1,0:T(8,128)(2,1)} %stack.2), calls=%async_computation | async-start | bytes 11796480 | tf_op jit(solution)/shard_map/all_to_all | solution.py:43
  18.3 96.7 %all-to-all-done = bf16[4,1,512,1440]{2,3,1,0:T(8,128)(2,1)} async-done(((bf16[4,1,512,1440]{2,3,1,0:T(8,128)(2,1)}), bf16[4,1,512,1440]{2,3,1,0:T(8,128)(2,1)}, u32[]{:S(2)}, u32[]{:S(2)}) %all-to-all-start) | async-done | bytes 5898272 | tf_op jit(solution)/shard_map/all_to_all | solution.py:43
  115.0 8.4 %copy.27 = bf16[4,1,512,1440]{3,2,0,1:T(8,128)(2,1)} copy(bf16[4,1,512,1440]{2,3,1,0:T(8,128)(2,1)} %all-to-all-done) | data formatting | bytes 11796480
  125.1 244.3 %while.20 = (s32[]{:T(128)}, bf16[64,1440]{1,0:T(8,128)(2,1)S(1)}, bf16[4,64,1440]{2,1,0:T(8,128)(2,1)}, bf16[4,64,512]{2,1,0:T(8,128)(2,1)}, s32[]{:T(128)}, /*...) while((s32[]{:T(128)}, bf16[64,1440]{1,0:T(8,128)(2,1)S(1)}, ...), condition=%wide.region_8.9_spmd.clone.clone, body=%wide.region_0.8_spmd.clone.clone.sunk | while | flops 958372544 | bytes 48405112 | solution.py:145
  138.2 7.3 %collective-permute-done.2 = bf16[64,1440]{1,0:T(8,128)(2,1)S(1)} collective-permute-done((bf16[64,1440]{1,0:T(8,128)(2,1)S(1)}, bf16[64,1440]{1,0:T(8,128)(2,1)S(1)}, u32[]{:S(2)}, u32[]{:S(2)}) %collective-permute-start.2) | collective-permute-done | bytes 184352 | tf_op jit(solution)/shard_map/while/body/eval_jaxpr/ppermute | solution.py:16
  150.1 3.0 collective-permute-start
  159.0 7.2 %collective-permute-done.2 = bf16[64,1440]{1,0:T(8,128)(2,1)S(1)} collective-permute-done((bf16[64,1440]{1,0:T(8,128)(2,1)S(1)}, bf16[64,1440]{1,0:T(8,128)(2,1)S(1)}, u32[]{:S(2)}, u32[]{:S(2)}) %collective-permute-start.2) | collective-permute-done | bytes 184352 | tf_op jit(solution)/shard_map/while/body/eval_jaxpr/ppermute | solution.py:16
  179.6 47.2 %collective-permute-done.2 = bf16[64,1440]{1,0:T(8,128)(2,1)S(1)} collective-permute-done((bf16[64,1440]{1,0:T(8,128)(2,1)S(1)}, bf16[64,1440]{1,0:T(8,128)(2,1)S(1)}, u32[]{:S(2)}, u32[]{:S(2)}) %collective-permute-start.2) | collective-permute-done | bytes 184352 | tf_op jit(solution)/shard_map/while/body/eval_jaxpr/ppermute | solution.py:16
  230.1 8.5 %conditional.8 = (bf16[64,2048]{1,0:T(8,128)(2,1)}, bf16[64,512]{1,0:T(8,128)(2,1)S(1)}, bf16[64,512]{0,1:T(8,128)(2,1)}) conditional(s32[]{:T(128)} %convert_element_type.69, () %tuple.82, (bf16[64,1440]{1,0:T(8,128)(2,1)S(1)}, f32[1,1440]{1,0:T(1,128)S(1)}, bf16[1440,2048]{1,0:T(8,128)(2,1)}, f32[64,1,32]{2,0,1:T(8,128)S(1)}, ...), branch_computations={%region_1.1_spmd, %region_2.3_spmd} | conditional | flops 474183744 | bytes 12898132 | solution.py:126
  232.3 3.9 %fusion.26 = f32[64,2048]{1,0:T(8,128)S(1)} fusion(bf16[1440,2048]{1,0:T(8,128)(2,1)} %get-tuple-element.374, bf16[64,1440]{1,0:T(8,128)(2,1)S(1)} %get-tuple-element.372, f32[1440]{0:T(1024)S(1)} %reduce, f32[64]{0:T(128)S(1)} %add_rsqrt_fusion), kind=kOutput, calls=%fused_computation.44 | convolution fusion | flops 377856000 | bytes 6612864 | tf_op jit(solution)/shard_map/while/body/eval_jaxpr/cond/branch_1_fun/dot_general | solution.py:67
  245.1 8.0 %conditional.9 = (bf16[64,1440]{1,0:T(8,128)(2,1)S(1)}) conditional(s32[]{:T(128)} %convert_element_type.69, bf16[64,1440]{1,0:T(8,128)(2,1)S(1)} %bitcast_select_fusion.5, (bf16[64,1440]{1,0:T(8,128)(2,1)S(1)}, bf16[64,512]{0,1:T(8,128)(2,1)S(1)}, bf16[64,512]{0,1:T(8,128)(2,1)S(1)}, bf16[64,512]{1,0:T(8,128)(2,1)S(1)}, s32[]{:T(128)}, ...), branch_computations={%region_4.4_spmd, %region_5.7_spmd} | conditional | flops 483969664 | bytes 32420688 | solution.py:128
  255.1 7.4 %collective-permute-done.2 = bf16[64,1440]{1,0:T(8,128)(2,1)S(1)} collective-permute-done((bf16[64,1440]{1,0:T(8,128)(2,1)S(1)}, bf16[64,1440]{1,0:T(8,128)(2,1)S(1)}, u32[]{:S(2)}, u32[]{:S(2)}) %collective-permute-start.2) | collective-permute-done | bytes 184352 | tf_op jit(solution)/shard_map/while/body/eval_jaxpr/ppermute | solution.py:16
  265.8 8.4 %conditional.8 = (bf16[64,2048]{1,0:T(8,128)(2,1)}, bf16[64,512]{1,0:T(8,128)(2,1)S(1)}, bf16[64,512]{0,1:T(8,128)(2,1)}) conditional(s32[]{:T(128)} %convert_element_type.69, () %tuple.82, (bf16[64,1440]{1,0:T(8,128)(2,1)S(1)}, f32[1,1440]{1,0:T(1,128)S(1)}, bf16[1440,2048]{1,0:T(8,128)(2,1)}, f32[64,1,32]{2,0,1:T(8,128)S(1)}, ...), branch_computations={%region_1.1_spmd, %region_2.3_spmd} | conditional | flops 474183744 | bytes 12898132 | solution.py:126
  268.0 3.9 %fusion.26 = f32[64,2048]{1,0:T(8,128)S(1)} fusion(bf16[1440,2048]{1,0:T(8,128)(2,1)} %get-tuple-element.374, bf16[64,1440]{1,0:T(8,128)(2,1)S(1)} %get-tuple-element.372, f32[1440]{0:T(1024)S(1)} %reduce, f32[64]{0:T(128)S(1)} %add_rsqrt_fusion), kind=kOutput, calls=%fused_computation.44 | convolution fusion | flops 377856000 | bytes 6612864 | tf_op jit(solution)/shard_map/while/body/eval_jaxpr/cond/branch_1_fun/dot_general | solution.py:67
  280.8 8.0 %conditional.9 = (bf16[64,1440]{1,0:T(8,128)(2,1)S(1)}) conditional(s32[]{:T(128)} %convert_element_type.69, bf16[64,1440]{1,0:T(8,128)(2,1)S(1)} %bitcast_select_fusion.5, (bf16[64,1440]{1,0:T(8,128)(2,1)S(1)}, bf16[64,512]{0,1:T(8,128)(2,1)S(1)}, bf16[64,512]{0,1:T(8,128)(2,1)S(1)}, bf16[64,512]{1,0:T(8,128)(2,1)S(1)}, s32[]{:T(128)}, ...), branch_computations={%region_4.4_spmd, %region_5.7_spmd} | conditional | flops 483969664 | bytes 32420688 | solution.py:128
  290.9 7.4 %collective-permute-done.2 = bf16[64,1440]{1,0:T(8,128)(2,1)S(1)} collective-permute-done((bf16[64,1440]{1,0:T(8,128)(2,1)S(1)}, bf16[64,1440]{1,0:T(8,128)(2,1)S(1)}, u32[]{:S(2)}, u32[]{:S(2)}) %collective-permute-start.2) | collective-permute-done | bytes 184352 | tf_op jit(solution)/shard_map/while/body/eval_jaxpr/ppermute | solution.py:16
  301.6 8.4 %conditional.8 = (bf16[64,2048]{1,0:T(8,128)(2,1)}, bf16[64,512]{1,0:T(8,128)(2,1)S(1)}, bf16[64,512]{0,1:T(8,128)(2,1)}) conditional(s32[]{:T(128)} %convert_element_type.69, () %tuple.82, (bf16[64,1440]{1,0:T(8,128)(2,1)S(1)}, f32[1,1440]{1,0:T(1,128)S(1)}, bf16[1440,2048]{1,0:T(8,128)(2,1)}, f32[64,1,32]{2,0,1:T(8,128)S(1)}, ...), branch_computations={%region_1.1_spmd, %region_2.3_spmd} | conditional | flops 474183744 | bytes 12898132 | solution.py:126
  303.7 3.9 %fusion.26 = f32[64,2048]{1,0:T(8,128)S(1)} fusion(bf16[1440,2048]{1,0:T(8,128)(2,1)} %get-tuple-element.374, bf16[64,1440]{1,0:T(8,128)(2,1)S(1)} %get-tuple-element.372, f32[1440]{0:T(1024)S(1)} %reduce, f32[64]{0:T(128)S(1)} %add_rsqrt_fusion), kind=kOutput, calls=%fused_computation.44 | convolution fusion | flops 377856000 | bytes 6612864 | tf_op jit(solution)/shard_map/while/body/eval_jaxpr/cond/branch_1_fun/dot_general | solution.py:67
  316.5 8.0 %conditional.9 = (bf16[64,1440]{1,0:T(8,128)(2,1)S(1)}) conditional(s32[]{:T(128)} %convert_element_type.69, bf16[64,1440]{1,0:T(8,128)(2,1)S(1)} %bitcast_select_fusion.5, (bf16[64,1440]{1,0:T(8,128)(2,1)S(1)}, bf16[64,512]{0,1:T(8,128)(2,1)S(1)}, bf16[64,512]{0,1:T(8,128)(2,1)S(1)}, bf16[64,512]{1,0:T(8,128)(2,1)S(1)}, s32[]{:T(128)}, ...), branch_computations={%region_4.4_spmd, %region_5.7_spmd} | conditional | flops 483969664 | bytes 32420688 | solution.py:128
  326.6 7.4 %collective-permute-done.2 = bf16[64,1440]{1,0:T(8,128)(2,1)S(1)} collective-permute-done((bf16[64,1440]{1,0:T(8,128)(2,1)S(1)}, bf16[64,1440]{1,0:T(8,128)(2,1)S(1)}, u32[]{:S(2)}, u32[]{:S(2)}) %collective-permute-start.2) | collective-permute-done | bytes 184352 | tf_op jit(solution)/shard_map/while/body/eval_jaxpr/ppermute | solution.py:16
  337.3 8.4 %conditional.8 = (bf16[64,2048]{1,0:T(8,128)(2,1)}, bf16[64,512]{1,0:T(8,128)(2,1)S(1)}, bf16[64,512]{0,1:T(8,128)(2,1)}) conditional(s32[]{:T(128)} %convert_element_type.69, () %tuple.82, (bf16[64,1440]{1,0:T(8,128)(2,1)S(1)}, f32[1,1440]{1,0:T(1,128)S(1)}, bf16[1440,2048]{1,0:T(8,128)(2,1)}, f32[64,1,32]{2,0,1:T(8,128)S(1)}, ...), branch_computations={%region_1.1_spmd, %region_2.3_spmd} | conditional | flops 474183744 | bytes 12898132 | solution.py:126
  339.5 3.9 %fusion.26 = f32[64,2048]{1,0:T(8,128)S(1)} fusion(bf16[1440,2048]{1,0:T(8,128)(2,1)} %get-tuple-element.374, bf16[64,1440]{1,0:T(8,128)(2,1)S(1)} %get-tuple-element.372, f32[1440]{0:T(1024)S(1)} %reduce, f32[64]{0:T(128)S(1)} %add_rsqrt_fusion), kind=kOutput, calls=%fused_computation.44 | convolution fusion | flops 377856000 | bytes 6612864 | tf_op jit(solution)/shard_map/while/body/eval_jaxpr/cond/branch_1_fun/dot_general | solution.py:67
  352.3 8.0 %conditional.9 = (bf16[64,1440]{1,0:T(8,128)(2,1)S(1)}) conditional(s32[]{:T(128)} %convert_element_type.69, bf16[64,1440]{1,0:T(8,128)(2,1)S(1)} %bitcast_select_fusion.5, (bf16[64,1440]{1,0:T(8,128)(2,1)S(1)}, bf16[64,512]{0,1:T(8,128)(2,1)S(1)}, bf16[64,512]{0,1:T(8,128)(2,1)S(1)}, bf16[64,512]{1,0:T(8,128)(2,1)S(1)}, s32[]{:T(128)}, ...), branch_computations={%region_4.4_spmd, %region_5.7_spmd} | conditional | flops 483969664 | bytes 32420688 | solution.py:128
  362.3 7.2 %collective-permute-done.2 = bf16[64,1440]{1,0:T(8,128)(2,1)S(1)} collective-permute-done((bf16[64,1440]{1,0:T(8,128)(2,1)S(1)}, bf16[64,1440]{1,0:T(8,128)(2,1)S(1)}, u32[]{:S(2)}, u32[]{:S(2)}) %collective-permute-start.2) | collective-permute-done | bytes 184352 | tf_op jit(solution)/shard_map/while/body/eval_jaxpr/ppermute | solution.py:16
  (300 shorter events, 133.3 us)
Async XLA Ops:
  7.2 116.2 %all-gather.2.cloned.1.call-start = ((), (), s32[]{:S(2)}) async-start(), calls=%async_computation.1 | async-start | bytes 7372800 | tf_op jit(solution)/shard_map/all_gather | solution.py:41
  11.5 103.4 %all-to-all-start = ((bf16[4,1,512,1440]{2,3,1,0:T(8,128)(2,1)}), bf16[4,1,512,1440]{2,3,1,0:T(8,128)(2,1)}, u32[]{:S(2)}, u32[]{:S(2)}) async-start(bf16[4,1,512,1440]{2,3,1,0:T(8,128)(2,1)} %stack.2), calls=%async_computation | async-start | bytes 11796480 | tf_op jit(solution)/shard_map/all_to_all | solution.py:43
  18.2 106.9 %copy-start = (bf16[1,1440,512]{2,1,0:T(8,128)(2,1)S(1)}, bf16[1,1440,512]{2,1,0:T(8,128)(2,1)}, u32[]{:S(2)}) copy-start(bf16[1,1440,512]{2,1,0:T(8,128)(2,1)} %param.19) | copy-start | bytes 4423684
  129.8 6.3 %collective-permute-start = (bf16[64,512]{0,1:T(8,128)(2,1)}, bf16[64,512]{0,1:T(8,128)(2,1)S(1)}, u32[]{:S(2)}, u32[]{:S(2)}) collective-permute-start(bf16[64,512]{0,1:T(8,128)(2,1)} %get-tuple-element.736), channel_id=1, source_target_pairs={{0,2},{1,3},{4,6},{5,7},{8,10},{9,11},{12,14},{13,15},{16,18},{17,... | collective-permute-start | bytes 196616 | tf_op jit(solution)/shard_map/while/body/eval_jaxpr/ppermute | solution.py:16
  132.1 4.0 %collective-permute-start.1 = (bf16[64,512]{0,1:T(8,128)(2,1)}, bf16[64,512]{0,1:T(8,128)(2,1)S(1)}, u32[]{:S(2)}, u32[]{:S(2)}) collective-permute-start(bf16[64,512]{0,1:T(8,128)(2,1)} %get-tuple-element.736), channel_id=1, source_target_pairs={{0,1},{1,2},{2,3},{4,5},{5,6},{6,7},{8,9},{9,10},{10,11},{12,13},{... | collective-permute-start | bytes 196616 | tf_op jit(solution)/shard_map/while/body/eval_jaxpr/ppermute | solution.py:16
  136.1 9.3 %collective-permute-start.2 = (bf16[64,1440]{1,0:T(8,128)(2,1)S(1)}, bf16[64,1440]{1,0:T(8,128)(2,1)S(1)}, u32[]{:S(2)}, u32[]{:S(2)}) collective-permute-start(bf16[64,1440]{1,0:T(8,128)(2,1)S(1)} %get-tuple-element.811), channel_id=1, source_target_pairs={{0,4},{4,8},{8,12},{1,5},{5,9},{9,13},{2,6},{6,10},{10,14},{3,7},{... | collective-permute-start | bytes 552968 | tf_op jit(solution)/shard_map/while/body/eval_jaxpr/ppermute | solution.py:16
  150.1 6.8 %collective-permute-start = (bf16[64,512]{0,1:T(8,128)(2,1)}, bf16[64,512]{0,1:T(8,128)(2,1)S(1)}, u32[]{:S(2)}, u32[]{:S(2)}) collective-permute-start(bf16[64,512]{0,1:T(8,128)(2,1)} %get-tuple-element.736), channel_id=1, source_target_pairs={{0,2},{1,3},{4,6},{5,7},{8,10},{9,11},{12,14},{13,15},{16,18},{17,... | collective-permute-start | bytes 196616 | tf_op jit(solution)/shard_map/while/body/eval_jaxpr/ppermute | solution.py:16
  153.1 3.8 collective-permute-start.1
  156.9 9.2 %collective-permute-start.2 = (bf16[64,1440]{1,0:T(8,128)(2,1)S(1)}, bf16[64,1440]{1,0:T(8,128)(2,1)S(1)}, u32[]{:S(2)}, u32[]{:S(2)}) collective-permute-start(bf16[64,1440]{1,0:T(8,128)(2,1)S(1)} %get-tuple-element.811), channel_id=1, source_target_pairs={{0,4},{4,8},{8,12},{1,5},{5,9},{9,13},{2,6},{6,10},{10,14},{3,7},{... | collective-permute-start | bytes 552968 | tf_op jit(solution)/shard_map/while/body/eval_jaxpr/ppermute | solution.py:16
  170.8 6.8 %collective-permute-start = (bf16[64,512]{0,1:T(8,128)(2,1)}, bf16[64,512]{0,1:T(8,128)(2,1)S(1)}, u32[]{:S(2)}, u32[]{:S(2)}) collective-permute-start(bf16[64,512]{0,1:T(8,128)(2,1)} %get-tuple-element.736), channel_id=1, source_target_pairs={{0,2},{1,3},{4,6},{5,7},{8,10},{9,11},{12,14},{13,15},{16,18},{17,... | collective-permute-start | bytes 196616 | tf_op jit(solution)/shard_map/while/body/eval_jaxpr/ppermute | solution.py:16
  173.8 3.8 collective-permute-start.1
  177.6 49.3 %collective-permute-start.2 = (bf16[64,1440]{1,0:T(8,128)(2,1)S(1)}, bf16[64,1440]{1,0:T(8,128)(2,1)S(1)}, u32[]{:S(2)}, u32[]{:S(2)}) collective-permute-start(bf16[64,1440]{1,0:T(8,128)(2,1)S(1)} %get-tuple-element.811), channel_id=1, source_target_pairs={{0,4},{4,8},{8,12},{1,5},{5,9},{9,13},{2,6},{6,10},{10,14},{3,7},{... | collective-permute-start | bytes 552968 | tf_op jit(solution)/shard_map/while/body/eval_jaxpr/ppermute | solution.py:16
  238.6 6.5 %collective-permute-start = (bf16[64,512]{0,1:T(8,128)(2,1)}, bf16[64,512]{0,1:T(8,128)(2,1)S(1)}, u32[]{:S(2)}, u32[]{:S(2)}) collective-permute-start(bf16[64,512]{0,1:T(8,128)(2,1)} %get-tuple-element.736), channel_id=1, source_target_pairs={{0,2},{1,3},{4,6},{5,7},{8,10},{9,11},{12,14},{13,15},{16,18},{17,... | collective-permute-start | bytes 196616 | tf_op jit(solution)/shard_map/while/body/eval_jaxpr/ppermute | solution.py:16
  241.3 3.8 collective-permute-start.1
  253.1 9.5 %collective-permute-start.2 = (bf16[64,1440]{1,0:T(8,128)(2,1)S(1)}, bf16[64,1440]{1,0:T(8,128)(2,1)S(1)}, u32[]{:S(2)}, u32[]{:S(2)}) collective-permute-start(bf16[64,1440]{1,0:T(8,128)(2,1)S(1)} %get-tuple-element.811), channel_id=1, source_target_pairs={{0,4},{4,8},{8,12},{1,5},{5,9},{9,13},{2,6},{6,10},{10,14},{3,7},{... | collective-permute-start | bytes 552968 | tf_op jit(solution)/shard_map/while/body/eval_jaxpr/ppermute | solution.py:16
  274.3 6.5 %collective-permute-start = (bf16[64,512]{0,1:T(8,128)(2,1)}, bf16[64,512]{0,1:T(8,128)(2,1)S(1)}, u32[]{:S(2)}, u32[]{:S(2)}) collective-permute-start(bf16[64,512]{0,1:T(8,128)(2,1)} %get-tuple-element.736), channel_id=1, source_target_pairs={{0,2},{1,3},{4,6},{5,7},{8,10},{9,11},{12,14},{13,15},{16,18},{17,... | collective-permute-start | bytes 196616 | tf_op jit(solution)/shard_map/while/body/eval_jaxpr/ppermute | solution.py:16
  277.0 3.8 collective-permute-start.1
  288.8 9.5 %collective-permute-start.2 = (bf16[64,1440]{1,0:T(8,128)(2,1)S(1)}, bf16[64,1440]{1,0:T(8,128)(2,1)S(1)}, u32[]{:S(2)}, u32[]{:S(2)}) collective-permute-start(bf16[64,1440]{1,0:T(8,128)(2,1)S(1)} %get-tuple-element.811), channel_id=1, source_target_pairs={{0,4},{4,8},{8,12},{1,5},{5,9},{9,13},{2,6},{6,10},{10,14},{3,7},{... | collective-permute-start | bytes 552968 | tf_op jit(solution)/shard_map/while/body/eval_jaxpr/ppermute | solution.py:16
  310.0 6.5 %collective-permute-start = (bf16[64,512]{0,1:T(8,128)(2,1)}, bf16[64,512]{0,1:T(8,128)(2,1)S(1)}, u32[]{:S(2)}, u32[]{:S(2)}) collective-permute-start(bf16[64,512]{0,1:T(8,128)(2,1)} %get-tuple-element.736), channel_id=1, source_target_pairs={{0,2},{1,3},{4,6},{5,7},{8,10},{9,11},{12,14},{13,15},{16,18},{17,... | collective-permute-start | bytes 196616 | tf_op jit(solution)/shard_map/while/body/eval_jaxpr/ppermute | solution.py:16
  312.8 3.8 collective-permute-start.1
  324.6 9.5 %collective-permute-start.2 = (bf16[64,1440]{1,0:T(8,128)(2,1)S(1)}, bf16[64,1440]{1,0:T(8,128)(2,1)S(1)}, u32[]{:S(2)}, u32[]{:S(2)}) collective-permute-start(bf16[64,1440]{1,0:T(8,128)(2,1)S(1)} %get-tuple-element.811), channel_id=1, source_target_pairs={{0,4},{4,8},{8,12},{1,5},{5,9},{9,13},{2,6},{6,10},{10,14},{3,7},{... | collective-permute-start | bytes 552968 | tf_op jit(solution)/shard_map/while/body/eval_jaxpr/ppermute | solution.py:16
  345.7 6.5 %collective-permute-start = (bf16[64,512]{0,1:T(8,128)(2,1)}, bf16[64,512]{0,1:T(8,128)(2,1)S(1)}, u32[]{:S(2)}, u32[]{:S(2)}) collective-permute-start(bf16[64,512]{0,1:T(8,128)(2,1)} %get-tuple-element.736), channel_id=1, source_target_pairs={{0,2},{1,3},{4,6},{5,7},{8,10},{9,11},{12,14},{13,15},{16,18},{17,... | collective-permute-start | bytes 196616 | tf_op jit(solution)/shard_map/while/body/eval_jaxpr/ppermute | solution.py:16
  348.5 3.8 collective-permute-start.1
  360.3 9.2 %collective-permute-start.2 = (bf16[64,1440]{1,0:T(8,128)(2,1)S(1)}, bf16[64,1440]{1,0:T(8,128)(2,1)S(1)}, u32[]{:S(2)}, u32[]{:S(2)}) collective-permute-start(bf16[64,1440]{1,0:T(8,128)(2,1)S(1)} %get-tuple-element.811), channel_id=1, source_target_pairs={{0,4},{4,8},{8,12},{1,5},{5,9},{9,13},{2,6},{6,10},{10,14},{3,7},{... | collective-permute-start | bytes 552968 | tf_op jit(solution)/shard_map/while/body/eval_jaxpr/ppermute | solution.py:16
  (21 other events, 371.9 us)
Sparse Core Ops, SparseCore 0:
  9.5 76.7 all-gather.1
